TPU v7x, 32 devices: a whole 2x2x4 slice. The times are simulated.
32 devices in a mesh: comm: 4 (over z), arc: 8 (over y, x, core).
Axes of the slice: x: 2, y: 2, z: 4, core: 2. Of those that a mesh axis runs over, the one named last changes fastest.
Arguments:
- prev_dist: float32 [512, 2048], P('comm', 'arc'), may hold values from 0 to 4
- source_node: int32 [512], P('comm'), may hold values from 0 to 2047, as said below
- arc_tail: int32 [16, 2048], P(None, 'arc'), may hold values from 0 to 2047, as said below
- base_cost: float32 [16, 2048], P(None, 'arc'), may hold values from 0.05 to 1
- arc_price: float32 [16, 2048], P(None, 'arc'), may hold values from 0 to 1
- capacity: float32 [16, 2048], P(None, 'arc')
- path_arcs: int32 [512, 128], P(('comm', 'arc')), may hold values from 0 to 32767, as said below
- demand: float32 [512], P(('comm', 'arc')), may hold values from 0.5 to 2
Outputs:
- final_dist: float32 [512, 2048], P('comm', 'arc')
- new_price: float32 [16, 2048], P(None, 'arc')
Inputs may be any that keep to these rules, and one draw needn't show every extreme that they name: `arc_tail`: the tail of arc s * 2048 + v lies in a node block (nodes 128 b to 128 b + 127) at most 2 blocks before or after v's block, counted around the cycle of blocks. Row k is a walk: the head of path_arcs[k, h + 1] (its id modulo 2048) is the tail of path_arcs[k, h]. `source_node`: the tail of path_arcs[k, 127].
All inputs are finite; a program needn't handle non-finite values.
Results may differ from a plain program's by a relative error of at most 0.00002.
Values sent between devices are 32-bit elements; how exact they have to be, the bound alone decides.
A program may use at most 64 MiB of HBM per device.

v0:
```python
import jax
import jax.numpy as jnp
from jax import lax
from jax.sharding import PartitionSpec as P

SWEEPS = 8


step_size = 0.25
eps_value = 1e-06


def with_halo(cells, sides, width):
    for axis, dim in sides:
        count = lax.axis_size(axis)
        head = lax.slice_in_dim(cells, 0, width, axis=dim)
        tail = lax.slice_in_dim(cells, cells.shape[dim] - width, cells.shape[dim], axis=dim)
        cells = jnp.concatenate(
            [
                lax.ppermute(tail, axis, [(i, (i + 1) % count) for i in range(count)]),
                cells,
                lax.ppermute(head, axis, [((i + 1) % count, i) for i in range(count)]),
            ],
            axis=dim,
        )
    return cells


def relax(window, window_start, tail_nodes, weights, current, node_count):
    degree = tail_nodes.shape[0]
    node_span = tail_nodes.shape[1]
    local_index = jnp.mod(tail_nodes - window_start, node_count).reshape(-1)
    picked = jnp.take(window, local_index, axis=0).reshape(degree, node_span, window.shape[1])
    candidate = picked + weights[:, :, None]
    return jnp.minimum(current, jnp.min(candidate, axis=0))


def shards(prev_dist, source_node, arc_tail, base_cost, arc_price, capacity, path_arcs, demand):
    shard_nodes = prev_dist.shape[1]
    arc_devices = lax.axis_size("arc")
    node_count = shard_nodes * arc_devices
    degree = arc_tail.shape[0]
    sweep_total = SWEEPS
    first_node = lax.axis_index("arc") * shard_nodes
    node_ids = first_node + jnp.arange(shard_nodes, dtype=jnp.int32)
    arc_weight = base_cost + arc_price
    node_major = jnp.where(node_ids[:, None] == source_node[None, :], jnp.float32(0.0), prev_dist.T)
    for sweep_number in range(sweep_total):
        window = with_halo(node_major, (("arc", 0),), shard_nodes)
        node_major = relax(
            window, first_node - shard_nodes, arc_tail, arc_weight, node_major, node_count
        )
    distance = node_major.T
    amounts = jnp.broadcast_to(demand[:, None], path_arcs.shape).reshape(-1)
    flattened = (
        jnp.zeros((degree * node_count,), jnp.float32).at[path_arcs.reshape(-1)].add(amounts)
    )
    partial_flow = lax.psum_scatter(
        flattened.reshape(degree, node_count), "arc", scatter_dimension=1, tiled=True
    )
    arc_flow = lax.psum(partial_flow, "comm")
    gradient = arc_flow - capacity
    square_sum = lax.psum(jnp.sum(gradient * gradient), "arc")
    scale_root = jnp.sqrt(square_sum / (degree * node_count) + eps_value)
    new_price = jnp.maximum(arc_price + step_size * gradient / scale_root, jnp.float32(0.0))
    return (distance, new_price)


def solution(mesh):
    in_specs = (
        P("comm", "arc"),
        P("comm"),
        P(None, "arc"),
        P(None, "arc"),
        P(None, "arc"),
        P(None, "arc"),
        P(("comm", "arc"), None),
        P(("comm", "arc")),
    )
    out_specs = (P("comm", "arc"), P(None, "arc"))
    return jax.shard_map(shards, mesh=mesh, in_specs=in_specs, out_specs=out_specs, check_vma=False)
```

profile of v0, /device:TPU:0, one launch (start us, length us, event | category | flops | bytes accessed | tf_op | source)
XLA Modules:
  0.0 245.0 jit_solution(11023003977533881316)
XLA Ops:
  9.0 3.4 %collective-permute-start.1 = (f32[256,128]{1,0:T(8,128)S(1)}, f32[256,128]{1,0:T(8,128)S(1)}, u32[]{:S(2)}, u32[]{:S(2)}) collective-permute-start(f32[256,128]{1,0:T(8,128)S(1)} %bitcast_select_fusion), channel_id=1, source_target_pairs={{1,0},{2,1},{3,2},{4,3},{5,4},{6,5},{7,6},{0,7},{9,8},{10,9},{11,1... | collective-permute-start | bytes 393224 | tf_op jit(solution)/shard_map/ppermute | solution.py:22
  13.2 11.3 %scatter_custom_fusion = f32[32768]{0:T(1024)S(1)} fusion(s32[2048]{0:T(1024)S(1)} %bitcast.60, f32[2048]{0:T(1024)S(1)} %broadcast_bitcast_fusion, f32[]{:T(128)} %constant.60.clone.1), kind=kCustom, calls=%fused_computation.42 | custom fusion | flops 2048 | bytes 131076 | tf_op jit(solution)/shard_map/scatter-add | solution.py:56
  26.1 14.1 %gather_fusion = f32[4096,128]{1,0:T(8,128)} fusion(f32[768,128]{1,0:T(8,128)S(1)} %pad_maximum_fusion, s32[4096]{0:T(1024)S(1)} %fusion.4), kind=kCustom, calls=%fused_computation.clone | custom fusion | bytes 4210688 | tf_op jit(solution)/shard_map/jit(_take)/gather | solution.py:33
  40.2 20.2 %reduce-scatter.2.cloned.1.call-done = f32[16,256]{1,0:T(8,128)} async-done(((f32[16,2048]{1,0:T(8,128)}), f32[16,256]{1,0:T(8,128)}) %reduce-scatter.2.cloned.1.call-update) | async-done | bytes 16400 | tf_op jit(solution)/shard_map/reduce_scatter | solution.py:58
  60.4 19.4 %psum.14 = f32[16,256]{1,0:T(8,128)S(1)} all-reduce(f32[16,256]{1,0:T(8,128)} %reduce-scatter.2.cloned.1.call-done), channel_id=1, replica_groups=mesh['comm'=4,'arc'=8] {'comm'}, use_global_device_ids=true, to_apply=%region_10.12 | all-reduce | flops 4096 | bytes 32768 | tf_op jit(solution)/shard_map/psum | solution.py:61
  80.4 3.6 %broadcast_select_fusion.7 = f32[4096,128]{1,0:T(8,128)S(1)} fusion(f32[4096,128]{1,0:T(8,128)} %gather_fusion, pred[4096]{0:T(1024)(128)(4,1)S(1)} %compare_and_fusion), kind=kLoop, calls=%fused_computation.24 | loop fusion | flops 524288 | bytes 4198400 | tf_op jit(solution)/shard_map/jit(_take)/select_n | solution.py:33
  84.0 12.5 %psum.15 = f32[]{:T(128)} all-reduce(f32[]{:T(128)} %multiply_reduce_fusion), channel_id=1, replica_groups=mesh['comm'=4,'arc'=8] {'arc'}, use_global_device_ids=true, to_apply=%region_12.14 | all-reduce | flops 1 | bytes 8 | tf_op jit(solution)/shard_map/psum | solution.py:63
  99.2 2.5 %collective-permute-done.3 = f32[256,128]{1,0:T(8,128)S(1)} collective-permute-done((f32[256,128]{1,0:T(8,128)S(1)}, f32[256,128]{1,0:T(8,128)S(1)}, u32[]{:S(2)}, u32[]{:S(2)}) %collective-permute-start.3) | collective-permute-done | bytes 131104 | tf_op jit(solution)/shard_map/ppermute | solution.py:22
  101.7 3.7 %collective-permute-done.2 = f32[256,128]{1,0:T(8,128)S(1)} collective-permute-done((f32[256,128]{1,0:T(8,128)S(1)}, f32[256,128]{1,0:T(8,128)S(1)}, u32[]{:S(2)}, u32[]{:S(2)}) %collective-permute-start.2) | collective-permute-done | bytes 131104 | tf_op jit(solution)/shard_map/ppermute | solution.py:20
  105.4 10.8 %gather_fusion.1 = f32[4096,128]{1,0:T(8,128)S(1)} fusion(f32[768,128]{1,0:T(8,128)S(1)} %pad_maximum_fusion.1, s32[4096]{0:T(1024)S(1)} %fusion.4), kind=kCustom, calls=%fused_computation.1.clone | custom fusion | bytes 4210688 | tf_op jit(solution)/shard_map/jit(_take)/gather | solution.py:33
  119.7 3.2 %collective-permute-done.5 = f32[256,128]{1,0:T(8,128)S(1)} collective-permute-done((f32[256,128]{1,0:T(8,128)S(1)}, f32[256,128]{1,0:T(8,128)S(1)}, u32[]{:S(2)}, u32[]{:S(2)}) %collective-permute-start.5) | collective-permute-done | bytes 131104 | tf_op jit(solution)/shard_map/ppermute | solution.py:22
  125.2 10.8 %gather_fusion.2 = f32[4096,128]{1,0:T(8,128)S(1)} fusion(f32[768,128]{1,0:T(8,128)S(1)} %pad_maximum_fusion.2, s32[4096]{0:T(1024)S(1)} %fusion.4), kind=kCustom, calls=%fused_computation.2.clone | custom fusion | bytes 4210688 | tf_op jit(solution)/shard_map/jit(_take)/gather | solution.py:33
  139.5 3.2 %collective-permute-done.7 = f32[256,128]{1,0:T(8,128)S(1)} collective-permute-done((f32[256,128]{1,0:T(8,128)S(1)}, f32[256,128]{1,0:T(8,128)S(1)}, u32[]{:S(2)}, u32[]{:S(2)}) %collective-permute-start.7) | collective-permute-done | bytes 131104 | tf_op jit(solution)/shard_map/ppermute | solution.py:22
  144.8 10.8 %gather_fusion.3 = f32[4096,128]{1,0:T(8,128)S(1)} fusion(f32[768,128]{1,0:T(8,128)S(1)} %pad_maximum_fusion.3, s32[4096]{0:T(1024)S(1)} %fusion.4), kind=kCustom, calls=%fused_computation.3.clone | custom fusion | bytes 4210688 | tf_op jit(solution)/shard_map/jit(_take)/gather | solution.py:33
  159.2 2.9 %collective-permute-done.9 = f32[256,128]{1,0:T(8,128)S(1)} collective-permute-done((f32[256,128]{1,0:T(8,128)S(1)}, f32[256,128]{1,0:T(8,128)S(1)}, u32[]{:S(2)}, u32[]{:S(2)}) %collective-permute-start.9) | collective-permute-done | bytes 131104 | tf_op jit(solution)/shard_map/ppermute | solution.py:22
  162.2 2.3 collective-permute-done.8
  164.6 10.8 %gather_fusion.4 = f32[4096,128]{1,0:T(8,128)S(1)} fusion(f32[768,128]{1,0:T(8,128)S(1)} %pad_maximum_fusion.4, s32[4096]{0:T(1024)S(1)} %fusion.4), kind=kCustom, calls=%fused_computation.4.clone | custom fusion | bytes 4210688 | tf_op jit(solution)/shard_map/jit(_take)/gather | solution.py:33
  178.8 3.2 %collective-permute-done.11 = f32[256,128]{1,0:T(8,128)S(1)} collective-permute-done((f32[256,128]{1,0:T(8,128)S(1)}, f32[256,128]{1,0:T(8,128)S(1)}, u32[]{:S(2)}, u32[]{:S(2)}) %collective-permute-start.11) | collective-permute-done | bytes 131104 | tf_op jit(solution)/shard_map/ppermute | solution.py:22
  184.1 10.8 %gather_fusion.5 = f32[4096,128]{1,0:T(8,128)S(1)} fusion(f32[768,128]{1,0:T(8,128)S(1)} %pad_maximum_fusion.5, s32[4096]{0:T(1024)S(1)} %fusion.4), kind=kCustom, calls=%fused_computation.5.clone | custom fusion | bytes 4210688 | tf_op jit(solution)/shard_map/jit(_take)/gather | solution.py:33
  198.6 2.9 %collective-permute-done.13 = f32[256,128]{1,0:T(8,128)S(1)} collective-permute-done((f32[256,128]{1,0:T(8,128)S(1)}, f32[256,128]{1,0:T(8,128)S(1)}, u32[]{:S(2)}, u32[]{:S(2)}) %collective-permute-start.13) | collective-permute-done | bytes 131104 | tf_op jit(solution)/shard_map/ppermute | solution.py:22
  201.5 2.3 collective-permute-done.12
  203.9 10.8 %gather_fusion.6 = f32[4096,128]{1,0:T(8,128)S(1)} fusion(f32[768,128]{1,0:T(8,128)S(1)} %pad_maximum_fusion.6, s32[4096]{0:T(1024)S(1)} %fusion.4), kind=kCustom, calls=%fused_computation.6.clone | custom fusion | bytes 4210688 | tf_op jit(solution)/shard_map/jit(_take)/gather | solution.py:33
  218.1 3.2 %collective-permute-done.15 = f32[256,128]{1,0:T(8,128)S(1)} collective-permute-done((f32[256,128]{1,0:T(8,128)S(1)}, f32[256,128]{1,0:T(8,128)S(1)}, u32[]{:S(2)}, u32[]{:S(2)}) %collective-permute-start.15) | collective-permute-done | bytes 131104 | tf_op jit(solution)/shard_map/ppermute | solution.py:22
  223.4 10.8 %gather_fusion.7 = f32[4096,128]{1,0:T(8,128)S(1)} fusion(f32[768,128]{1,0:T(8,128)S(1)} %pad_maximum_fusion.7, s32[4096]{0:T(1024)S(1)} %fusion.4), kind=kCustom, calls=%fused_computation.7.clone | custom fusion | bytes 4210688 | tf_op jit(solution)/shard_map/jit(_take)/gather | solution.py:33
  (85 shorter events, 40.3 us)
Async XLA Ops:
  7.2 6.0 %copy-start = (f32[16]{0:T(128)S(1)}, f32[16]{0:T(128)}, u32[]{:S(2)}) copy-start(f32[16]{0:T(128)} %param.17) | copy-start | bytes 196
  7.2 53.2 %reduce-scatter.2.cloned.1.call-start = ((), (), s32[]{:S(2)}) async-start(), calls=%async_computation.1 | async-start | bytes 147456 | tf_op jit(solution)/shard_map/reduce_scatter | solution.py:58
  9.0 17.0 %collective-permute-start.1 = (f32[256,128]{1,0:T(8,128)S(1)}, f32[256,128]{1,0:T(8,128)S(1)}, u32[]{:S(2)}, u32[]{:S(2)}) collective-permute-start(f32[256,128]{1,0:T(8,128)S(1)} %bitcast_select_fusion), channel_id=1, source_target_pairs={{1,0},{2,1},{3,2},{4,3},{5,4},{6,5},{7,6},{0,7},{9,8},{10,9},{11,1... | collective-permute-start | bytes 393224 | tf_op jit(solution)/shard_map/ppermute | solution.py:22
  12.4 13.6 %collective-permute-start = (f32[256,128]{1,0:T(8,128)S(1)}, f32[256,128]{1,0:T(8,128)S(1)}, u32[]{:S(2)}, u32[]{:S(2)}) collective-permute-start(f32[256,128]{1,0:T(8,128)S(1)} %bitcast_select_fusion), channel_id=1, source_target_pairs={{0,1},{1,2},{2,3},{3,4},{4,5},{5,6},{6,7},{7,0},{8,9},{9,10},{10,1... | collective-permute-start | bytes 393224 | tf_op jit(solution)/shard_map/ppermute | solution.py:20
  26.1 53.7 %copy-start.5 = (f32[16,256]{1,0:T(8,128)S(1)}, f32[16,256]{1,0:T(8,128)}, u32[]{:S(2)}) copy-start(f32[16,256]{1,0:T(8,128)} %param.15) | copy-start | bytes 49156
  80.4 16.8 %copy-start.6 = (f32[16,256]{1,0:T(8,128)S(1)}, f32[16,256]{1,0:T(8,128)}, u32[]{:S(2)}) copy-start(f32[16,256]{1,0:T(8,128)} %param.14) | copy-start | bytes 49156
  80.4 16.8 %copy-start.7 = (f32[16,256]{1,0:T(8,128)S(1)}, f32[16,256]{1,0:T(8,128)}, u32[]{:S(2)}) copy-start(f32[16,256]{1,0:T(8,128)} %param.13) | copy-start | bytes 49156
  84.0 14.5 %copy-start.8 = (s32[128]{0:T(128)S(1)}, s32[128]{0:T(128)}, u32[]{:S(2)}) copy-start(s32[128]{0:T(128)} %param.11) | copy-start | bytes 1540
  98.5 17.7 %copy-start.3 = (f32[256,128]{1,0:T(8,128)}, f32[256,128]{1,0:T(8,128)S(1)}, u32[]{:S(2)}) copy-start(f32[256,128]{1,0:T(8,128)S(1)} %add_reduce_fusion.7) | copy-start | bytes 393220
  98.6 3.0 %collective-permute-start.3 = (f32[256,128]{1,0:T(8,128)S(1)}, f32[256,128]{1,0:T(8,128)S(1)}, u32[]{:S(2)}, u32[]{:S(2)}) collective-permute-start(f32[256,128]{1,0:T(8,128)S(1)} %fusion.5), channel_id=1, source_target_pairs={{1,0},{2,1},{3,2},{4,3},{5,4},{6,5},{7,6},{0,7},{9,8},{10,9},{11,1... | collective-permute-start | bytes 393224 | tf_op jit(solution)/shard_map/ppermute | solution.py:22
  98.7 6.7 %collective-permute-start.2 = (f32[256,128]{1,0:T(8,128)S(1)}, f32[256,128]{1,0:T(8,128)S(1)}, u32[]{:S(2)}, u32[]{:S(2)}) collective-permute-start(f32[256,128]{1,0:T(8,128)S(1)} %fusion.5), channel_id=1, source_target_pairs={{0,1},{1,2},{2,3},{3,4},{4,5},{5,6},{6,7},{7,0},{8,9},{9,10},{10,1... | collective-permute-start | bytes 393224 | tf_op jit(solution)/shard_map/ppermute | solution.py:20
  119.1 3.8 %collective-permute-start.5 = (f32[256,128]{1,0:T(8,128)S(1)}, f32[256,128]{1,0:T(8,128)S(1)}, u32[]{:S(2)}, u32[]{:S(2)}) collective-permute-start(f32[256,128]{1,0:T(8,128)S(1)} %min.49), channel_id=1, source_target_pairs={{1,0},{2,1},{3,2},{4,3},{5,4},{6,5},{7,6},{0,7},{9,8},{10,9},{11,1... | collective-permute-start | bytes 393224 | tf_op jit(solution)/shard_map/ppermute | solution.py:22
  119.2 6.0 %collective-permute-start.4 = (f32[256,128]{1,0:T(8,128)S(1)}, f32[256,128]{1,0:T(8,128)S(1)}, u32[]{:S(2)}, u32[]{:S(2)}) collective-permute-start(f32[256,128]{1,0:T(8,128)S(1)} %min.49), channel_id=1, source_target_pairs={{0,1},{1,2},{2,3},{3,4},{4,5},{5,6},{6,7},{7,0},{8,9},{9,10},{10,1... | collective-permute-start | bytes 393224 | tf_op jit(solution)/shard_map/ppermute | solution.py:20
  138.9 3.8 %collective-permute-start.7 = (f32[256,128]{1,0:T(8,128)S(1)}, f32[256,128]{1,0:T(8,128)S(1)}, u32[]{:S(2)}, u32[]{:S(2)}) collective-permute-start(f32[256,128]{1,0:T(8,128)S(1)} %min.51), channel_id=1, source_target_pairs={{1,0},{2,1},{3,2},{4,3},{5,4},{6,5},{7,6},{0,7},{9,8},{10,9},{11,1... | collective-permute-start | bytes 393224 | tf_op jit(solution)/shard_map/ppermute | solution.py:22
  139.4 5.3 %collective-permute-start.6 = (f32[256,128]{1,0:T(8,128)S(1)}, f32[256,128]{1,0:T(8,128)S(1)}, u32[]{:S(2)}, u32[]{:S(2)}) collective-permute-start(f32[256,128]{1,0:T(8,128)S(1)} %min.51), channel_id=1, source_target_pairs={{0,1},{1,2},{2,3},{3,4},{4,5},{5,6},{6,7},{7,0},{8,9},{9,10},{10,1... | collective-permute-start | bytes 393224 | tf_op jit(solution)/shard_map/ppermute | solution.py:20
  158.4 3.8 %collective-permute-start.9 = (f32[256,128]{1,0:T(8,128)S(1)}, f32[256,128]{1,0:T(8,128)S(1)}, u32[]{:S(2)}, u32[]{:S(2)}) collective-permute-start(f32[256,128]{1,0:T(8,128)S(1)} %min.53), channel_id=1, source_target_pairs={{1,0},{2,1},{3,2},{4,3},{5,4},{6,5},{7,6},{0,7},{9,8},{10,9},{11,1... | collective-permute-start | bytes 393224 | tf_op jit(solution)/shard_map/ppermute | solution.py:22
  159.2 5.3 %collective-permute-start.8 = (f32[256,128]{1,0:T(8,128)S(1)}, f32[256,128]{1,0:T(8,128)S(1)}, u32[]{:S(2)}, u32[]{:S(2)}) collective-permute-start(f32[256,128]{1,0:T(8,128)S(1)} %min.53), channel_id=1, source_target_pairs={{0,1},{1,2},{2,3},{3,4},{4,5},{5,6},{6,7},{7,0},{8,9},{9,10},{10,1... | collective-permute-start | bytes 393224 | tf_op jit(solution)/shard_map/ppermute | solution.py:20
  178.2 3.8 %collective-permute-start.11 = (f32[256,128]{1,0:T(8,128)S(1)}, f32[256,128]{1,0:T(8,128)S(1)}, u32[]{:S(2)}, u32[]{:S(2)}) collective-permute-start(f32[256,128]{1,0:T(8,128)S(1)} %min.55), channel_id=1, source_target_pairs={{1,0},{2,1},{3,2},{4,3},{5,4},{6,5},{7,6},{0,7},{9,8},{10,9},{11,1... | collective-permute-start | bytes 393224 | tf_op jit(solution)/shard_map/ppermute | solution.py:22
  178.7 5.3 %collective-permute-start.10 = (f32[256,128]{1,0:T(8,128)S(1)}, f32[256,128]{1,0:T(8,128)S(1)}, u32[]{:S(2)}, u32[]{:S(2)}) collective-permute-start(f32[256,128]{1,0:T(8,128)S(1)} %min.55), channel_id=1, source_target_pairs={{0,1},{1,2},{2,3},{3,4},{4,5},{5,6},{6,7},{7,0},{8,9},{9,10},{10,1... | collective-permute-start | bytes 393224 | tf_op jit(solution)/shard_map/ppermute | solution.py:20
  197.7 6.1 %copy-start.1 = (f32[256,128]{1,0:T(8,128)}, f32[256,128]{1,0:T(8,128)S(1)}, u32[]{:S(2)}) copy-start(f32[256,128]{1,0:T(8,128)S(1)} %add_reduce_fusion.2) | copy-start | bytes 393220
  197.7 3.8 %collective-permute-start.13 = (f32[256,128]{1,0:T(8,128)S(1)}, f32[256,128]{1,0:T(8,128)S(1)}, u32[]{:S(2)}, u32[]{:S(2)}) collective-permute-start(f32[256,128]{1,0:T(8,128)S(1)} %min.57), channel_id=1, source_target_pairs={{1,0},{2,1},{3,2},{4,3},{5,4},{6,5},{7,6},{0,7},{9,8},{10,9},{11,1... | collective-permute-start | bytes 393224 | tf_op jit(solution)/shard_map/ppermute | solution.py:22
  198.5 5.3 %collective-permute-start.12 = (f32[256,128]{1,0:T(8,128)S(1)}, f32[256,128]{1,0:T(8,128)S(1)}, u32[]{:S(2)}, u32[]{:S(2)}) collective-permute-start(f32[256,128]{1,0:T(8,128)S(1)} %min.57), channel_id=1, source_target_pairs={{0,1},{1,2},{2,3},{3,4},{4,5},{5,6},{6,7},{7,0},{8,9},{9,10},{10,1... | collective-permute-start | bytes 393224 | tf_op jit(solution)/shard_map/ppermute | solution.py:20
  217.5 3.8 %collective-permute-start.15 = (f32[256,128]{1,0:T(8,128)S(1)}, f32[256,128]{1,0:T(8,128)S(1)}, u32[]{:S(2)}, u32[]{:S(2)}) collective-permute-start(f32[256,128]{1,0:T(8,128)S(1)} %min.59), channel_id=1, source_target_pairs={{1,0},{2,1},{3,2},{4,3},{5,4},{6,5},{7,6},{0,7},{9,8},{10,9},{11,1... | collective-permute-start | bytes 393224 | tf_op jit(solution)/shard_map/ppermute | solution.py:22
  218.1 5.3 %collective-permute-start.14 = (f32[256,128]{1,0:T(8,128)S(1)}, f32[256,128]{1,0:T(8,128)S(1)}, u32[]{:S(2)}, u32[]{:S(2)}) collective-permute-start(f32[256,128]{1,0:T(8,128)S(1)} %min.59), channel_id=1, source_target_pairs={{0,1},{1,2},{2,3},{3,4},{4,5},{5,6},{6,7},{7,0},{8,9},{9,10},{10,1... | collective-permute-start | bytes 393224 | tf_op jit(solution)/shard_map/ppermute | solution.py:20
  (2 other events, 1.9 us)
Sparse Core Ops, SparseCore 0:
  25.3 35.0 reduce-scatter.1
where the time goes:
time: 245 us
  local copies, waits for them, and re-layouts  92.3 us (38%)
  waiting for transfers between devices  58.3 us (24%)
  other arithmetic  39.5 us (16%)
  blocking collectives  31.8 us (13%)
  between operations  15.2 us (6%)
  starting transfers between devices  7.89 us (3%)
    gather x8, local copies, waits for them, and re-layouts, relax(): jnp.take(window, local_index, axis=0)  89.5 us
    ppermute x8, waiting for transfers between devices, with_halo(): lax.ppermute(head, axis, [((i + 1) % count, i) for i in range(count)])  21.2 us
    reduce_scatter x1, waiting for transfers between devices, shards(): lax.psum_scatter(flattened.reshape(degree, node_count), 'arc', scatter_di...  20.2 us
    psum x1, blocking collectives, shards(): arc_flow = lax.psum(partial_flow, 'comm')  19.4 us
    select_n x8, other arithmetic, relax(): jnp.take(window, local_index, axis=0)  18.6 us
    ppermute x8, waiting for transfers between devices, with_halo(): lax.ppermute(tail, axis, [(i, (i + 1) % count) for i in range(count)])  16.9 us
    psum x1, blocking collectives, shards(): square_sum = lax.psum(jnp.sum(gradient * gradient), 'arc')  12.5 us
    scatter-add x1, other arithmetic, shards(): jnp.zeros((degree * node_count,), jnp.float32).at[path_arcs.reshape(-1)]  11.3 us
  transfers between devices with their start and end apart: 17, of which 15 were waited for; matrix products, arithmetic and copies ran while one was open for 11% of the time, Pallas kernels for 0%

commit v1 on v0

v1 whole, which is shorter than its diff:
```python
import functools

import jax
import jax.numpy as jnp
from jax import lax
from jax.experimental import pallas as pl
from jax.experimental.pallas import tpu as pltpu
from jax.sharding import PartitionSpec as P

SWEEPS = 8
LANES = 128
REACH = 2
UNROLL = 2

step_size = 0.25
eps_value = 1e-06
MESH_ID = pl.DeviceIdType.MESH


def kernel(A, C, m,
           source_ref, demand_ref, dist_ref, tail_ref, cost_ref, price_ref, cap_ref, path_ref,
           out_ref, newp_ref,
           D, T, W, CODE, F, RF, G, Q,
           d_s, d_r, t_s, t_r, w_s, w_r, f_s, f_r, g_s, g_r, q_s, q_r, o_s, o_r):
    rows = D.shape[2]
    degree, span = tail_ref.shape
    NB = A * m
    node_count = NB * LANES
    me = lax.axis_index("arc")
    mc = lax.axis_index("comm")

    def arc_dev(i):
        return lax.rem(me + i, A)

    def comm_dev(i):
        return lax.rem(mc + i, C)

    W[me] = cost_ref[...] + price_ref[...]
    T[me] = tail_ref[...]
    D[0, me] = dist_ref[me]

    barrier = pltpu.get_barrier_semaphore()
    for i in range(1, A):
        pl.semaphore_signal(barrier, inc=1, device_id=(mc, arc_dev(i)), device_id_type=MESH_ID)
    for i in range(1, C):
        pl.semaphore_signal(barrier, inc=1, device_id=(comm_dev(i), me), device_id_type=MESH_ID)
    pl.semaphore_wait(barrier, A - 1 + C - 1)

    def send(src, dst, ss, rs, dev):
        return pltpu.make_async_remote_copy(src_ref=src, dst_ref=dst, send_sem=ss, recv_sem=rs,
                                            device_id=dev, device_id_type=MESH_ID)

    bulk = []
    for i in range(1, A):
        j = arc_dev(i)
        dev = (mc, j)
        bulk.append(send(tail_ref, T.at[me], t_s.at[i - 1], t_r.at[i - 1], dev))
        bulk.append(send(dist_ref.at[j], D.at[0, me], d_s.at[i - 1], d_r.at[i - 1], dev))
        bulk.append(send(W.at[me], W.at[me], w_s.at[i - 1], w_r.at[i - 1], dev))
    for c in bulk:
        c.start()

    total_rows = NB * degree
    shift_nodes = (node_count - 1).bit_length()
    assert 1 << shift_nodes == node_count
    path = path_ref[...]
    slot_of = path >> shift_nodes
    node_of = path & (node_count - 1)
    row_of = (node_of >> 7) * degree + slot_of
    lane_of = node_of & (LANES - 1)
    row_iota = lax.broadcasted_iota(jnp.int32, (total_rows, LANES), 0)
    lane_iota = lax.broadcasted_iota(jnp.int32, (LANES, LANES), 0)
    acc = jnp.zeros((total_rows, LANES), jnp.float32)
    for k in range(path.shape[0]):
        hi = jnp.where(row_iota == row_of[k:k + 1, :], 1.0, 0.0).astype(jnp.bfloat16)
        lo = jnp.where(lane_iota == lane_of[k:k + 1, :], 1.0, 0.0).astype(jnp.bfloat16)
        count = lax.dot_general(hi, lo, (((1,), (1,)), ((), ())), preferred_element_type=jnp.float32)
        acc = acc + count * demand_ref[k]
    F[...] = acc.reshape(F.shape)

    for c in bulk:
        c.wait_recv()

    sub_iota = lax.broadcasted_iota(jnp.int32, (rows, LANES), 0)
    lane_row = lax.broadcasted_iota(jnp.int32, (rows, LANES), 1)
    source = jnp.zeros((rows, LANES), jnp.int32)
    for r in range(rows):
        source = jnp.where(sub_iota == r, source_ref[me * rows + r], source)
    def prepare(j, _):
        for h in range(m):
            lanes = slice(h * LANES, (h + 1) * LANES)
            vb = j * m + h
            D[0, j, :, lanes] = jnp.where(lane_row + vb * LANES == source, 0.0, D[0, j, :, lanes])
            tail = T[j, :, lanes]
            rel = (tail >> 7) - vb + REACH
            rel = jnp.where(rel < 0, rel + NB, rel)
            rel = jnp.where(rel >= NB, rel - NB, rel)
            CODE[j, :, lanes] = rel
            T[j, :, lanes] = tail & (LANES - 1)
        return 0

    for c in bulk:
        c.wait_send()
    lax.fori_loop(0, A, prepare, 0)

    flows = []
    for i in range(1, A):
        j = arc_dev(i)
        flows.append(send(F.at[j], RF.at[me], f_s.at[i - 1], f_r.at[i - 1], (mc, j)))
    for c in flows:
        c.start()

    chunks = [slice(r, min(r + 8, rows)) for r in range(0, rows, 8)]

    def relax_block(read, write, j):
        for h in range(m):
            lanes = slice(h * LANES, (h + 1) * LANES)
            srcs = []
            for off in range(-REACH, REACH + 1):
                q = h + off
                jj = lax.rem(j + (q // m) % A, A)
                blk = q % m
                srcs.append([D[read, jj, ch, blk * LANES:(blk + 1) * LANES] for ch in chunks])
            best = list(srcs[REACH])
            for s in range(degree):
                for n, ch in enumerate(chunks):
                    shape = best[n].shape
                    idx = jnp.broadcast_to(T[j, s:s + 1, lanes], shape)
                    code = jnp.broadcast_to(CODE[j, s:s + 1, lanes], shape)
                    w = jnp.broadcast_to(W[j, s:s + 1, lanes], shape)
                    got = [jnp.take_along_axis(srcs[b][n], idx, axis=1, mode="promise_in_bounds")
                           for b in range(2 * REACH + 1)]
                    pick = got[2 * REACH]
                    for b in range(2 * REACH):
                        pick = jnp.where(code == b, got[b], pick)
                    best[n] = jnp.minimum(best[n], pick + w)
            for n, ch in enumerate(chunks):
                D[write, j, ch, lanes] = best[n]

    def sweeps(first, last):
        def one(t, _):
            read = lax.rem(t, 2)
            def blk(j, _):
                relax_block(read, 1 - read, j)
                return 0
            lax.fori_loop(0, A, blk, 0, unroll=UNROLL)
            return 0
        lax.fori_loop(first, last, one, 0)

    sweeps(0, 2)
    for c in flows:
        c.wait()
    total = F[me]
    for i in range(1, A):
        total = total + RF[arc_dev(i)]
    G[mc] = total
    sweeps(2, 3)
    groups = [send(G.at[mc], G.at[mc], g_s.at[i - 1], g_r.at[i - 1], (comm_dev(i), me)) for i in range(1, C)]
    for c in groups:
        c.start()
    sweeps(3, 5)
    for c in groups:
        c.wait()
    flow = G[0]
    for i in range(1, C):
        flow = flow + G[i]
    gradient = [flow[h * degree:(h + 1) * degree, :] - cap_ref[:, h * LANES:(h + 1) * LANES] for h in range(m)]
    square = sum(g * g for g in gradient)
    Q[me] = square
    sweeps(5, 6)
    norms = [send(Q.at[me], Q.at[me], q_s.at[i - 1], q_r.at[i - 1], (mc, arc_dev(i))) for i in range(1, A)]
    for c in norms:
        c.start()
    sweeps(6, SWEEPS - 1)
    for c in norms:
        c.wait()
    square = Q[0]
    for i in range(1, A):
        square = square + Q[i]
    scale_root = jnp.sqrt(jnp.sum(square) / (degree * node_count) + eps_value)
    for h in range(m):
        lanes = slice(h * LANES, (h + 1) * LANES)
        newp_ref[:, lanes] = jnp.maximum(price_ref[:, lanes] + step_size * gradient[h] / scale_root, 0.0)

    read = (SWEEPS - 1) % 2
    outs = [send(D.at[1 - read, arc_dev(i)], out_ref.at[me], o_s.at[i - 1], o_r.at[i - 1], (mc, arc_dev(i)))
            for i in range(1, A)]
    for i in range(1, A + 1):
        relax_block(read, 1 - read, arc_dev(i))
        if i >= 2:
            outs[i - 2].start()
    out_ref[me] = D[1 - read, me]
    for c in outs:
        c.wait()


def shards(A, C, prev_dist, source_node, arc_tail, base_cost, arc_price, capacity, path_arcs, demand):
    commodities, span = prev_dist.shape
    degree = arc_tail.shape[0]
    rows = commodities // A
    m = span // LANES
    f32 = jnp.float32
    vmem = pl.BlockSpec(memory_space=pltpu.VMEM)
    smem = pl.BlockSpec(memory_space=pltpu.SMEM)
    sems = pltpu.SemaphoreType.DMA
    out, new_price = pl.pallas_call(
        functools.partial(kernel, A, C, m),
        out_shape=(jax.ShapeDtypeStruct((A, rows, span), f32), jax.ShapeDtypeStruct((degree, span), f32)),
        in_specs=[smem, smem] + [vmem] * 6,
        out_specs=(vmem, vmem),
        scratch_shapes=[
            pltpu.VMEM((2, A, rows, span), f32),
            pltpu.VMEM((A, degree, span), jnp.int32),
            pltpu.VMEM((A, degree, span), f32),
            pltpu.VMEM((A, degree, span), jnp.int32),
            pltpu.VMEM((A, m * degree, LANES), f32),
            pltpu.VMEM((A, m * degree, LANES), f32),
            pltpu.VMEM((C, m * degree, LANES), f32),
            pltpu.VMEM((A, degree, LANES), f32),
        ] + [sems((A - 1,))] * 8 + [sems((C - 1,))] * 2 + [sems((A - 1,))] * 4,
        compiler_params=pltpu.CompilerParams(collective_id=0, has_side_effects=True),
    )(source_node, demand, prev_dist.reshape(A, rows, span), arc_tail, base_cost, arc_price, capacity, path_arcs)
    return (out.reshape(commodities, span), new_price)


def solution(mesh):
    in_specs = (
        P("comm", "arc"),
        P("comm"),
        P(None, "arc"),
        P(None, "arc"),
        P(None, "arc"),
        P(None, "arc"),
        P(("comm", "arc"), None),
        P(("comm", "arc")),
    )
    out_specs = (P("comm", "arc"), P(None, "arc"))
    body = functools.partial(shards, mesh.shape["arc"], mesh.shape["comm"])
    return jax.shard_map(body, mesh=mesh, in_specs=in_specs, out_specs=out_specs, check_vma=False)
```

time: 245 us -> 55.9 us (0.23)
  local copies, waits for them, and re-layouts: 92.3 us -> 2.18 us
  waiting for transfers between devices: 58.3 us -> 0 us
  Pallas kernels: 0 us -> 52.9 us
  other arithmetic: 39.5 us -> 0 us
  blocking collectives: 31.8 us -> 0 us
  between operations: 15.2 us -> 0.65 us
  starting transfers between devices: 7.89 us -> 0 us
    gather x8 -> x0, local copies, waits for them, and re-layouts: 89.5 us -> none  [relax(): jnp.take(window, local_index, axis=0)]
    pallas_call x0 -> x1, Pallas kernels: none -> 52.9 us  [shards(): pl.pallas_call(functools.partial(kernel, A, C, m), out_shape=(jax.ShapeDt...]
    ppermute x16 -> x0, waiting for transfers between devices: 38.1 us -> none  [the longest x8 21.2 us: with_halo(): lax.ppermute(head, axis, [((i + 1) % count, i) for i in range(count)])]
    psum x2 -> x0, blocking collectives: 31.8 us -> none  [the longest x1 19.4 us: shards(): arc_flow = lax.psum(partial_flow, 'comm')]
    reduce_scatter x1 -> x0, waiting for transfers between devices: 20.2 us -> none  [shards(): lax.psum_scatter(flattened.reshape(degree, node_count), 'arc', scatter_di...]
    select_n x10 -> x0, other arithmetic: 20.1 us -> none  [the longest x8 18.6 us: relax(): jnp.take(window, local_index, axis=0)]
    scatter-add x1 -> x0, other arithmetic: 11.3 us -> none  [shards(): jnp.zeros((degree * node_count,), jnp.float32).at[path_arcs.reshape(-1)]]
    ppermute x16 -> x0, starting transfers between devices: 7.85 us -> none  [the longest x8 6.71 us: with_halo(): lax.ppermute(head, axis, [((i + 1) % count, i) for i in range(count)])]
  transfers between devices with their start and end apart: 17 -> 0, of which waited for: 15 -> 0; matrix products, arithmetic and copies ran while one was open for 11% -> 0% of each run, Pallas kernels for 0% -> 0%
where the time goes in v1:
time: 55.9 us; the launch traced here: 55.7 us
  Pallas kernels  52.9 us (95%)
  local copies, waits for them, and re-layouts  2.18 us (4%)
  between operations  0.65 us (1%)
    pallas_call x1, Pallas kernels, shards(): pl.pallas_call(functools.partial(kernel, A, C, m), out_shape=(jax.ShapeDt...  52.9 us
    unnamed x4, local copies, waits for them, and re-layouts  2.18 us

profile of v1, /device:TPU:0, one launch (start us, length us, event | category | flops | bytes accessed | tf_op | source)
XLA Modules:
  0.0 55.7 jit_solution(18085204479570255190)
XLA Ops:
  0.6 52.9 %shard_map.95 = (f32[8,16,256]{2,1,0:T(8,128)}, f32[16,256]{1,0:T(8,128)}) custom-call(s32[128]{0:T(128)} %source_ref.1, f32[16]{0:T(128)} %demand_ref.1, f32[8,16,256]{2,1,0:T(8,128)} %bitcast.2, s32[16,256]{1,0:T(8,128)} %tail_ref.1, f32[16,256]{1,0:T(8,128)} %cost_ref.1, f32[16,256]{1,0:T(8,128)} %price_ref.1, f32[16,256]{1,0:T(8,128)} %cap_ref.1, ...), custom_call_target="tpu_custom_call" | custom-call | tf_op jit(solution)/shard_map/pallas_call | solution.py:206
  53.6 0.0 copy-start
  53.6 1.6 %copy.12 = f32[128,256]{1,0:T(8,128)} copy(f32[128,256]{1,0:T(8,128)} %bitcast.3) | data formatting | bytes 262144
  55.1 0.0 copy-done
  55.1 0.6 %copy.13 = f32[16,256]{1,0:T(8,128)} copy(f32[16,256]{1,0:T(8,128)S(1)} %copy-done) | data formatting | bytes 32768
Async XLA Ops:
  53.6 1.6 %copy-start = (f32[16,256]{1,0:T(8,128)S(1)}, f32[16,256]{1,0:T(8,128)}, u32[]{:S(2)}) copy-start(f32[16,256]{1,0:T(8,128)} %get-tuple-element.9) | copy-start | bytes 49156

commit v2 on v1

--- a/solution.py
+++ b/solution.py
@@ -110,32 +110,50 @@
     for c in flows:
         c.start()
 
-    chunks = [slice(r, min(r + 8, rows)) for r in range(0, rows, 8)]
+    sub8 = lax.broadcasted_iota(jnp.int32, (8, LANES), 0)
+    halves = [(sub8 & d) == 0 for d in (4, 2, 1)]
+
+    def min_over_slots(parts):
+        parts = parts + [parts[-1]] * (8 - len(parts))
+        for mask, d in zip(halves, (4, 2, 1)):
+            merged = []
+            for lower, upper in zip(parts[:d], parts[d:]):
+                kept = jnp.where(mask, lower, upper)
+                other = jnp.where(mask, upper, lower)
+                moved = pltpu.roll(other, d, 0)
+                if d != 4:
+                    moved = jnp.where(mask, pltpu.roll(other, 8 - d, 0), moved)
+                merged.append(jnp.minimum(kept, moved))
+            parts = merged
+        return parts[0]
 
     def relax_block(read, write, j):
         for h in range(m):
             lanes = slice(h * LANES, (h + 1) * LANES)
-            srcs = []
+            where_from = []
             for off in range(-REACH, REACH + 1):
                 q = h + off
-                jj = lax.rem(j + (q // m) % A, A)
                 blk = q % m
-                srcs.append([D[read, jj, ch, blk * LANES:(blk + 1) * LANES] for ch in chunks])
-            best = list(srcs[REACH])
-            for s in range(degree):
-                for n, ch in enumerate(chunks):
-                    shape = best[n].shape
-                    idx = jnp.broadcast_to(T[j, s:s + 1, lanes], shape)
-                    code = jnp.broadcast_to(CODE[j, s:s + 1, lanes], shape)
-                    w = jnp.broadcast_to(W[j, s:s + 1, lanes], shape)
-                    got = [jnp.take_along_axis(srcs[b][n], idx, axis=1, mode="promise_in_bounds")
-                           for b in range(2 * REACH + 1)]
+                where_from.append((lax.rem(j + (q // m) % A, A), slice(blk * LANES, (blk + 1) * LANES)))
+            groups = [slice(g, g + 8) for g in range(0, degree, 8)]
+            idx = [T[j, g, lanes] for g in groups]
+            weight = [W[j, g, lanes] for g in groups]
+            code = [CODE[j, g, lanes] for g in groups]
+            masks = [[c == b for b in range(2 * REACH)] for c in code]
+            cand = [None] * rows
+            for g in range(len(groups)):
+                for r in range(rows):
+                    srcs = [jnp.broadcast_to(D[read, jj, r:r + 1, bl], (8, LANES)) for jj, bl in where_from]
+                    got = [jnp.take_along_axis(x, idx[g], axis=1, mode="promise_in_bounds") for x in srcs]
                     pick = got[2 * REACH]
                     for b in range(2 * REACH):
-                        pick = jnp.where(code == b, got[b], pick)
-                    best[n] = jnp.minimum(best[n], pick + w)
-            for n, ch in enumerate(chunks):
-                D[write, j, ch, lanes] = best[n]
+                        pick = jnp.where(masks[g][b], got[b], pick)
+                    pick = pick + weight[g]
+                    cand[r] = pick if cand[r] is None else jnp.minimum(cand[r], pick)
+            for first in range(0, rows, 8):
+                last = min(first + 8, rows)
+                best = min_over_slots(cand[first:last])[:last - first]
+                D[write, j, first:last, lanes] = jnp.minimum(D[read, j, first:last, lanes], best)
 
     def sweeps(first, last):
         def one(t, _):

time: 55.9 us -> 51.8 us (0.927)
  Pallas kernels: 52.9 us -> 48.8 us
    pallas_call x1, Pallas kernels: 52.9 us -> 48.8 us  [shards(): pl.pallas_call(functools.partial(kernel, A, C, m), out_shape=(jax.ShapeDt...]
where the time goes in v2:
time: 51.8 us; the launch traced here: 51.7 us
  Pallas kernels  48.8 us (94%)
  local copies, waits for them, and re-layouts  2.18 us (4%)
  between operations  0.65 us (1%)
    pallas_call x1, Pallas kernels, shards(): pl.pallas_call(functools.partial(kernel, A, C, m), out_shape=(jax.ShapeDt...  48.8 us
    unnamed x4, local copies, waits for them, and re-layouts  2.18 us

profile of v2, /device:TPU:0, one launch (start us, length us, event | category | flops | bytes accessed | tf_op | source)
XLA Modules:
  0.0 51.7 jit_solution(11295289456315747654)
XLA Ops:
  0.6 48.8 %shard_map.95 = (f32[8,16,256]{2,1,0:T(8,128)}, f32[16,256]{1,0:T(8,128)}) custom-call(s32[128]{0:T(128)} %source_ref.1, f32[16]{0:T(128)} %demand_ref.1, f32[8,16,256]{2,1,0:T(8,128)} %bitcast.2, s32[16,256]{1,0:T(8,128)} %tail_ref.1, f32[16,256]{1,0:T(8,128)} %cost_ref.1, f32[16,256]{1,0:T(8,128)} %price_ref.1, f32[16,256]{1,0:T(8,128)} %cap_ref.1, ...), custom_call_target="tpu_custom_call" | custom-call | tf_op jit(solution)/shard_map/pallas_call | solution.py:224
  49.5 0.0 copy-start
  49.5 1.6 %copy.12 = f32[128,256]{1,0:T(8,128)} copy(f32[128,256]{1,0:T(8,128)} %bitcast.3) | data formatting | bytes 262144
  51.1 0.0 copy-done
  51.1 0.6 %copy.13 = f32[16,256]{1,0:T(8,128)} copy(f32[16,256]{1,0:T(8,128)S(1)} %copy-done) | data formatting | bytes 32768
Async XLA Ops:
  49.5 1.6 %copy-start = (f32[16,256]{1,0:T(8,128)S(1)}, f32[16,256]{1,0:T(8,128)}, u32[]{:S(2)}) copy-start(f32[16,256]{1,0:T(8,128)} %get-tuple-element.9) | copy-start | bytes 49156

commit v3 on v2

--- a/solution.py
+++ b/solution.py
@@ -10,7 +10,7 @@
 SWEEPS = 8
 LANES = 128
 REACH = 2
-UNROLL = 2
+UNROLL = 4
 
 step_size = 0.25
 eps_value = 1e-06
@@ -127,7 +127,7 @@
             parts = merged
         return parts[0]
 
-    def relax_block(read, write, j):
+    def relax_block(read, write, j, pending):
         for h in range(m):
             lanes = slice(h * LANES, (h + 1) * LANES)
             where_from = []
@@ -140,28 +140,45 @@
             weight = [W[j, g, lanes] for g in groups]
             code = [CODE[j, g, lanes] for g in groups]
             masks = [[c == b for b in range(2 * REACH)] for c in code]
-            cand = [None] * rows
-            for g in range(len(groups)):
-                for r in range(rows):
-                    srcs = [jnp.broadcast_to(D[read, jj, r:r + 1, bl], (8, LANES)) for jj, bl in where_from]
-                    got = [jnp.take_along_axis(x, idx[g], axis=1, mode="promise_in_bounds") for x in srcs]
-                    pick = got[2 * REACH]
-                    for b in range(2 * REACH):
-                        pick = jnp.where(masks[g][b], got[b], pick)
-                    pick = pick + weight[g]
-                    cand[r] = pick if cand[r] is None else jnp.minimum(cand[r], pick)
-            for first in range(0, rows, 8):
+            for n, first in enumerate(range(0, rows, 8)):
                 last = min(first + 8, rows)
-                best = min_over_slots(cand[first:last])[:last - first]
-                D[write, j, first:last, lanes] = jnp.minimum(D[read, j, first:last, lanes], best)
+                got = {}
+                order = range(len(groups)) if n % 2 == 0 else range(len(groups) - 1, -1, -1)
+                for g in order:
+                    for r in range(first, last):
+                        got[g, r] = [jnp.take_along_axis(
+                            jnp.broadcast_to(D[read, jj, r:r + 1, bl], (8, LANES)), idx[g],
+                            axis=1, mode="promise_in_bounds") for jj, bl in where_from]
+                old = D[read, j, first:last, lanes]
+                if pending:
+                    pending.pop()()
+
+                def finish(got=got, order=order, masks=masks, weight=weight, first=first, last=last,
+                           old=old, j=j, lanes=lanes):
+                    cand = {}
+                    for g in order:
+                        for r in range(first, last):
+                            pick = got[g, r][2 * REACH]
+                            for b in range(2 * REACH):
+                                pick = jnp.where(masks[g][b], got[g, r][b], pick)
+                            pick = pick + weight[g]
+                            cand[r] = jnp.minimum(cand[r], pick) if r in cand else pick
+                    best = min_over_slots([cand[r] for r in range(first, last)])[:last - first]
+                    D[write, j, first:last, lanes] = jnp.minimum(old, best)
+
+                pending.append(finish)
 
     def sweeps(first, last):
         def one(t, _):
             read = lax.rem(t, 2)
-            def blk(j, _):
-                relax_block(read, 1 - read, j)
+            def blk(jo, _):
+                pending = []
+                for u in range(UNROLL):
+                    relax_block(read, 1 - read, jo * UNROLL + u, pending)
+                pending.pop()()
                 return 0
-            lax.fori_loop(0, A, blk, 0, unroll=UNROLL)
+            assert A % UNROLL == 0
+            lax.fori_loop(0, A // UNROLL, blk, 0)
             return 0
         lax.fori_loop(first, last, one, 0)
 
@@ -204,7 +221,9 @@
     outs = [send(D.at[1 - read, arc_dev(i)], out_ref.at[me], o_s.at[i - 1], o_r.at[i - 1], (mc, arc_dev(i)))
             for i in range(1, A)]
     for i in range(1, A + 1):
-        relax_block(read, 1 - read, arc_dev(i))
+        pending = []
+        relax_block(read, 1 - read, arc_dev(i), pending)
+        pending.pop()()
         if i >= 2:
             outs[i - 2].start()
     out_ref[me] = D[1 - read, me]

time: 51.8 us -> 47.6 us (0.919)
  Pallas kernels: 48.8 us -> 44.6 us
    pallas_call x1, Pallas kernels: 48.8 us -> 44.6 us  [shards(): pl.pallas_call(functools.partial(kernel, A, C, m), out_shape=(jax.ShapeDt...]
where the time goes in v3:
time: 47.6 us; the launch traced here: 47.4 us
  Pallas kernels  44.6 us (94%)
  local copies, waits for them, and re-layouts  2.18 us (5%)
  between operations  0.65 us (1%)
    pallas_call x1, Pallas kernels, shards(): pl.pallas_call(functools.partial(kernel, A, C, m), out_shape=(jax.ShapeDt...  44.6 us
    unnamed x4, local copies, waits for them, and re-layouts  2.18 us

profile of v3, /device:TPU:0, one launch (start us, length us, event | category | flops | bytes accessed | tf_op | source)
XLA Modules:
  0.0 47.4 jit_solution(5294641680146023384)
XLA Ops:
  0.6 44.6 %shard_map.95 = (f32[8,16,256]{2,1,0:T(8,128)}, f32[16,256]{1,0:T(8,128)}) custom-call(s32[128]{0:T(128)} %source_ref.1, f32[16]{0:T(128)} %demand_ref.1, f32[8,16,256]{2,1,0:T(8,128)} %bitcast.2, s32[16,256]{1,0:T(8,128)} %tail_ref.1, f32[16,256]{1,0:T(8,128)} %cost_ref.1, f32[16,256]{1,0:T(8,128)} %price_ref.1, f32[16,256]{1,0:T(8,128)} %cap_ref.1, ...), custom_call_target="tpu_custom_call" | custom-call | tf_op jit(solution)/shard_map/pallas_call | solution.py:243
  45.2 0.0 copy-start
  45.2 1.6 %copy.12 = f32[128,256]{1,0:T(8,128)} copy(f32[128,256]{1,0:T(8,128)} %bitcast.3) | data formatting | bytes 262144
  46.8 0.0 copy-done
  46.8 0.6 %copy.13 = f32[16,256]{1,0:T(8,128)} copy(f32[16,256]{1,0:T(8,128)S(1)} %copy-done) | data formatting | bytes 32768
Async XLA Ops:
  45.2 1.6 %copy-start = (f32[16,256]{1,0:T(8,128)S(1)}, f32[16,256]{1,0:T(8,128)}, u32[]{:S(2)}) copy-start(f32[16,256]{1,0:T(8,128)} %get-tuple-element.9) | copy-start | bytes 49156
